TPU v7x, 32 devices: a whole 2x2x4 slice. The times are simulated.
32 devices in a mesh: blk: 8 (over z, y), plane: 4 (over x, core).
Axes of the slice: x: 2, y: 2, z: 4, core: 2. Of those that a mesh axis runs over, the one named last changes fastest.
Arguments:
- tiles: bfloat16 [128, 24, 128, 128], P(('blk', 'plane')), may hold values from -0.25 to 0.25
- tile_cols: int32 [128, 24], P(('blk', 'plane')), may hold values from 0 to 511
- tile_count: int32 [128], P(('blk', 'plane')), may hold values from 18 to 24, as said below
- u_start: float32 [16384], P(('blk', 'plane')), may hold values from -0.046875 to 0.046875
- v_start: float32 [65536], P(('blk', 'plane')), may hold values from -0.0234375 to 0.0234375
- beta_start: float32 [1], replicated, may hold values from 0.5 to 1.5
- left_basis: float32 [16384, 128], P(('blk', 'plane')), may hold values from -0.046875 to 0.046875
- right_basis: float32 [65536, 128], P(('blk', 'plane')), may hold values from -0.0234375 to 0.0234375
Outputs:
- left_vectors: float32 [1, 16384], P(None, ('blk', 'plane'))
- right_vectors: float32 [1, 65536], P(None, ('blk', 'plane'))
- coefficients: float32 [2], replicated
Inputs may be any that keep to these rules, and one draw needn't show every extreme that they name: `tile_count`: slots at and after a row block's count are padding; some row block uses all 24 slots.
All inputs are finite; a program needn't handle non-finite values.
Results may differ from a plain program's by a relative error of at most 0.00055.
The roundings to bfloat16 on the way count: a program that leaves them out, or rounds other values in their place, can miss the bound.
Values may be sent and summed in bfloat16 or wider, within the bound.
A program may use at most 64 MiB of HBM per device.

v0:
```python
import functools
import math

import jax
import jax.numpy as jnp
from jax import lax
from jax.experimental import pallas as pl
from jax.experimental.pallas import tpu as pltpu
from jax.sharding import PartitionSpec as P

AXES = ("blk", "plane")
LANES = 128
NT_DIMS = (((1,), (1,)), ((), ()))
MAIN_VMEM = 67043328


def steps_kernel(
    devices,
    planes,
    own_tiles,
    left_scale,
    right_scale,
    beta_ref,
    count_ref,
    cols_ref,
    u_ref,
    v_ref,
    tiles_hbm,
    left_hbm,
    right_hbm,
    out_ref,
    tiles,
    left,
    right,
    left_t,
    right_t,
    v_send,
    v_all,
    cols_rows,
    pick_hot,
    put_hot,
    picked,
    contrib,
    gram_send,
    gram_recv,
    gram_sum,
    gram_all,
    gram_scr,
    dot_send,
    dot_recv,
    part_send,
    part_recv,
    own_scr,
    p_scr,
    copy_sem,
    send_sem,
    recv_sem,
):
    blocks, slots = cols_ref.shape
    keep = left.shape[1]
    me_blk, me_plane = lax.axis_index("blk"), lax.axis_index("plane")
    me = me_blk * planes + me_plane
    chunks, rows = gram_send.shape[1:3]
    pad_tiles = v_send.shape[0]
    part_rows = part_send.shape[1]
    stride = picked.shape[0] // blocks

    def target(step):
        other = lax.rem(me + step, devices)
        return other, (other // planes, lax.rem(other, planes))

    barrier = pltpu.get_barrier_semaphore()

    def greet(step, carry):
        _, place = target(step)
        pl.semaphore_signal(
            barrier, inc=1, device_id=place, device_id_type=pl.DeviceIdType.MESH
        )
        return carry

    lax.fori_loop(1, devices, greet, 0)

    loads = [
        pltpu.make_async_copy(left_hbm, left, copy_sem.at[0]),
        pltpu.make_async_copy(right_hbm, right, copy_sem.at[1]),
        pltpu.make_async_copy(tiles_hbm, tiles, copy_sem.at[2]),
    ]
    for load in loads:
        load.start()

    def send_all(phase, source, landing):
        def body(step, carry):
            other, place = target(step)
            pltpu.make_async_remote_copy(
                src_ref=source(other),
                dst_ref=landing.at[me],
                send_sem=send_sem.at[phase],
                recv_sem=recv_sem.at[phase],
                device_id=place,
                device_id_type=pl.DeviceIdType.MESH,
            ).start()
            return carry

        lax.fori_loop(1, devices, body, 0)

    def wait_all(sem, phase, landing):
        most = landing.at[pl.ds(0, devices - 1)]
        pltpu.make_async_copy(most, most, sem.at[phase]).wait()

    eye = lax.broadcasted_iota(jnp.int32, (LANES, LANES), 0) == lax.broadcasted_iota(
        jnp.int32, (LANES, LANES), 1
    )

    def to_col(row):
        return jnp.sum(jnp.where(eye, row, 0.0), axis=1, keepdims=True)

    def to_row(col):
        return jnp.sum(jnp.where(eye, col, 0.0), axis=0, keepdims=True)

    rounded = v_ref[...].astype(jnp.bfloat16)
    if pad_tiles > own_tiles:
        rounded = jnp.concatenate(
            [v_ref[...], jnp.zeros((pad_tiles - own_tiles, LANES), jnp.float32)], axis=0
        ).astype(jnp.bfloat16)
    v_send[...] = rounded
    v_all[me] = rounded
    cols_rows[...] = jnp.full(cols_rows.shape, -1.0, jnp.float32)
    for r in range(blocks):
        row = cols_ref[r : r + 1, :]
        alive = lax.broadcasted_iota(jnp.int32, (1, slots), 1) < count_ref[r]
        cols_rows[r : r + 1, 0:slots] = jnp.where(alive, row, -1).astype(jnp.float32)
    entries = picked.shape[0]
    lane = lax.broadcasted_iota(jnp.int32, (1, entries), 1)
    line = jnp.full((1, entries), -1.0, jnp.float32)
    for r in range(blocks):
        row = cols_rows[r : r + 1, :]
        if r:
            row = pltpu.roll(row, r * stride, 1)
        line = jnp.where((lane >= r * stride) & (lane < r * stride + slots), row, line)
    whole = line.astype(jnp.int32)
    pick_row = jnp.where(whole < 0, -1, whole // own_tiles * pad_tiles + whole % own_tiles)
    put_row = jnp.where(whole < 0, -1, whole // own_tiles * part_rows + whole % own_tiles)
    pick_col = to_col(pick_row.astype(jnp.float32)).astype(jnp.int32)
    pick_hot[...] = jnp.where(
        lax.broadcasted_iota(jnp.int32, pick_hot.shape, 1) == pick_col, 1.0, 0.0
    ).astype(jnp.bfloat16)
    put_hot[...] = jnp.where(
        lax.broadcasted_iota(jnp.int32, put_hot.shape, 0) == put_row, 1.0, 0.0
    ).astype(jnp.bfloat16)
    contrib[...] = jnp.zeros_like(contrib)

    def start_gram(side, basis_t, phase):
        whole = basis_t[...]
        high = whole.astype(jnp.bfloat16)
        rest = whole - high.astype(jnp.float32)
        mid = rest.astype(jnp.bfloat16)
        low = (rest - mid.astype(jnp.float32)).astype(jnp.bfloat16)

        def product(a, b):
            return lax.dot_general(a, b, NT_DIMS, preferred_element_type=jnp.float32)

        cross = product(high, mid) + product(high, low)
        gram = product(high, high) + (cross + cross.T + product(mid, mid))
        for c in range(chunks):
            gram_send[side, c] = gram[c * rows : (c + 1) * rows, :]
        gram_recv[side, me] = gram_send[side, lax.rem(me, chunks)]

    def share_gram(side, phase):
        wait_all(recv_sem, phase, gram_recv.at[side])
        mine = jnp.sum(gram_recv[side], axis=0)
        gram_sum[side] = mine
        gram_all[side, me] = mine
        send_all(phase + 1, lambda other: gram_sum.at[side], gram_all.at[side])

    def finish_gram(side, phase):
        wait_all(recv_sem, phase + 1, gram_all.at[side])
        for c in range(chunks):
            gram_scr[c * rows : (c + 1) * rows, :] = gram_all[side, c]
        return gram_scr[...]

    def send_gram(side, phase):
        send_all(
            phase, lambda other: gram_send.at[side, lax.rem(other, chunks)], gram_recv.at[side]
        )

    loads[0].wait()
    for r in range(left.shape[0] // LANES):
        left_t[:, r * LANES : (r + 1) * LANES] = left[r * LANES : (r + 1) * LANES, :].T
    start_gram(0, left_t, 1)
    pl.semaphore_wait(barrier, devices - 1)
    send_all(0, lambda other: v_send, v_all)
    send_gram(0, 1)


    loads[1].wait()
    for t in range(own_tiles):
        right_t[:, t * LANES : (t + 1) * LANES] = right[t * LANES : (t + 1) * LANES, :].T
    start_gram(1, right_t, 6)

    wait_all(recv_sem, 0, v_all)
    picked[...] = jnp.dot(
        pick_hot[...],
        v_all[...].reshape(devices * pad_tiles, LANES),
        preferred_element_type=jnp.float32,
    )
    loads[2].wait()
    beta = beta_ref[0]

    def forward(r, carry):
        total = jnp.zeros((LANES, LANES), jnp.float32)
        for s in range(slots):
            total = total + tiles[r, s].astype(jnp.float32) * picked[pl.ds(r * stride + s, 1), :]
        q = to_row(jnp.sum(total, axis=1, keepdims=True))
        p_scr[pl.ds(r, 1), :] = q - beta * u_ref[pl.ds(r, 1), :]
        return carry

    lax.fori_loop(0, blocks, forward, 0)

    def start_dots(phase, basis_t, vec, count):
        total = jnp.zeros((keep, LANES), jnp.float32)
        for r in range(count):
            total = total + basis_t[:, r * LANES : (r + 1) * LANES] * vec[r : r + 1, :]
        dots = to_row(jnp.sum(total, axis=1, keepdims=True))
        square = jnp.sum(vec * vec, keepdims=True)
        both = jnp.concatenate([dots, jnp.broadcast_to(square, (1, LANES))], axis=0)
        side = phase // 4
        dot_send[side] = both
        dot_recv[side, me] = both
        send_all(phase, lambda other: dot_send.at[side], dot_recv.at[side])

    def finish_dots(phase, gram):
        side = phase // 4
        wait_all(recv_sem, phase, dot_recv.at[side])
        both = jnp.sum(dot_recv[side], axis=0)
        first, square = both[0:1, :], both[1:2, 0:1]
        coef = 2.0 * to_col(first) - jnp.sum(gram * first, axis=1, keepdims=True)
        coef_row = to_row(coef)
        spread = jnp.sum(gram * coef_row, axis=1, keepdims=True)
        total = (
            square
            - 2.0 * jnp.sum(coef_row * first, keepdims=True)
            + jnp.sum(coef * spread, keepdims=True)
        )
        return coef, jnp.sqrt(total + 1e-06)

    p = p_scr[0:blocks, :]
    start_dots(3, left_t, p, blocks)

    share_gram(0, 1)
    send_gram(1, 6)

    coef, alpha = finish_dots(3, finish_gram(0, 1))
    for r in range(blocks):
        fix = jnp.sum(left_t[:, r * LANES : (r + 1) * LANES] * coef, axis=0, keepdims=True)
        p_scr[r : r + 1, :] = (p[r : r + 1, :] - fix) / alpha
    out_ref[own_tiles : own_tiles + blocks, :] = p_scr[0:blocks, :] * left_scale

    def backward(r, carry):
        row = p_scr[pl.ds(r, 1), :].astype(jnp.bfloat16).astype(jnp.float32)
        col = jnp.broadcast_to(to_col(row), (LANES, LANES))
        for g in range(0, slots, 8):
            lines = [
                jnp.sum(tiles[r, s].astype(jnp.float32) * col, axis=0, keepdims=True)
                for s in range(g, min(g + 8, slots))
            ]
            contrib[pl.ds(pl.multiple_of(r * stride + g, 8), len(lines)), :] = jnp.concatenate(
                lines, axis=0
            )
        return carry

    lax.fori_loop(0, blocks, backward, 0)
    rest = contrib[...]
    spread = jnp.zeros((devices * part_rows, LANES), jnp.float32)
    for _ in range(3):
        piece = rest.astype(jnp.bfloat16)
        rest = rest - piece.astype(jnp.float32)
        spread = spread + jnp.dot(put_hot[...], piece, preferred_element_type=jnp.float32)
    part_send[...] = spread.reshape(devices, part_rows, LANES)
    part_recv[me] = part_send[me]
    send_all(5, lambda other: part_send.at[other], part_recv)
    share_gram(1, 6)
    wait_all(recv_sem, 5, part_recv)
    own_scr[...] = jnp.sum(part_recv[...], axis=0)
    r_vec = own_scr[0:own_tiles, :] - alpha * v_ref[...]
    start_dots(4, right_t, r_vec, own_tiles)
    coef, beta_new = finish_dots(4, finish_gram(1, 6))
    place = lax.broadcasted_iota(jnp.int32, (1, LANES), 1)
    out_ref[own_tiles + blocks : own_tiles + blocks + 1, :] = jnp.where(
        place == 0, alpha, beta_new
    )
    for t in range(own_tiles):
        fix = jnp.sum(right_t[:, t * LANES : (t + 1) * LANES] * coef, axis=0, keepdims=True)
        out_ref[t : t + 1, :] = (r_vec[t : t + 1, :] - fix) / beta_new * right_scale

    wait_all(send_sem, 0, v_all)
    for phase, side in ((1, 0), (6, 1)):
        wait_all(send_sem, phase, gram_recv.at[side])
        wait_all(send_sem, phase + 1, gram_all.at[side])
    wait_all(send_sem, 3, dot_recv.at[0])
    wait_all(send_sem, 4, dot_recv.at[1])
    wait_all(send_sem, 5, part_recv)


def place_kernel(own_tiles, blocks, packed, out_left, out_right, out_coef):
    for r in range(blocks):
        out_left[:, r * LANES : (r + 1) * LANES] = packed[own_tiles + r : own_tiles + r + 1, :]
    for t in range(own_tiles):
        out_right[:, t * LANES : (t + 1) * LANES] = packed[t : t + 1, :]
    out_coef[...] = packed[own_tiles + blocks, 0:2]


def on_device(tiles, tile_cols, tile_count, u_start, v_start, beta_start, left_basis, right_basis):
    devices = lax.axis_size(AXES)
    planes = lax.axis_size("plane")
    blocks, slots = tile_cols.shape
    own_tiles = v_start.shape[0] // LANES
    left_rows, keep = left_basis.shape
    right_rows = right_basis.shape[0]
    pad_tiles = -(-own_tiles // 16) * 16
    part_rows = -(-own_tiles // 8) * 8
    rows = max(4, keep // devices)
    chunks = keep // rows
    stride = -(-slots // 8) * 8
    while (blocks * stride) % LANES:
        stride += 8
    entries = blocks * stride
    f32, bf16 = jnp.float32, jnp.bfloat16
    vmem = pl.BlockSpec(memory_space=pltpu.VMEM)
    smem = pl.BlockSpec(memory_space=pltpu.SMEM)
    hbm = pl.BlockSpec(memory_space=pl.ANY)
    packed = pl.pallas_call(
        functools.partial(
            steps_kernel,
            devices,
            planes,
            own_tiles,
            math.sqrt(left_rows * devices),
            math.sqrt(right_rows * devices),
        ),
        out_shape=jax.ShapeDtypeStruct((own_tiles + blocks + 1, LANES), f32),
        in_specs=[smem, smem, vmem, vmem, vmem, hbm, hbm, hbm],
        out_specs=vmem,
        scratch_shapes=[
            pltpu.VMEM(tiles.shape, bf16),
            pltpu.VMEM(left_basis.shape, f32),
            pltpu.VMEM(right_basis.shape, f32),
            pltpu.VMEM((keep, left_rows), f32),
            pltpu.VMEM((keep, right_rows), f32),
            pltpu.VMEM((pad_tiles, LANES), bf16),
            pltpu.VMEM((devices, pad_tiles, LANES), bf16),
            pltpu.VMEM((-(-blocks // 8) * 8, entries), f32),
            pltpu.VMEM((entries, devices * pad_tiles), bf16),
            pltpu.VMEM((devices * part_rows, entries), bf16),
            pltpu.VMEM((entries, LANES), f32),
            pltpu.VMEM((entries, LANES), f32),
            pltpu.VMEM((2, chunks, rows, keep), f32),
            pltpu.VMEM((2, devices, rows, keep), f32),
            pltpu.VMEM((2, rows, keep), f32),
            pltpu.VMEM((2, devices, rows, keep), f32),
            pltpu.VMEM((keep, keep), f32),
            pltpu.VMEM((2, 2, keep), f32),
            pltpu.VMEM((2, devices, 2, keep), f32),
            pltpu.VMEM((devices, part_rows, LANES), f32),
            pltpu.VMEM((devices, part_rows, LANES), f32),
            pltpu.VMEM((part_rows, LANES), f32),
            pltpu.VMEM((-(-blocks // 8) * 8, LANES), f32),
            pltpu.SemaphoreType.DMA((3,)),
            pltpu.SemaphoreType.DMA((8,)),
            pltpu.SemaphoreType.DMA((8,)),
        ],
        compiler_params=pltpu.CompilerParams(
            collective_id=0, has_side_effects=True, vmem_limit_bytes=MAIN_VMEM
        ),
    )(
        beta_start,
        tile_count,
        tile_cols,
        u_start.reshape(blocks, LANES),
        v_start.reshape(own_tiles, LANES),
        tiles,
        left_basis,
        right_basis,
    )
    return pl.pallas_call(
        functools.partial(place_kernel, own_tiles, blocks),
        out_shape=(
            jax.ShapeDtypeStruct((1, left_rows), f32),
            jax.ShapeDtypeStruct((1, right_rows), f32),
            jax.ShapeDtypeStruct((2,), f32),
        ),
        in_specs=[vmem],
        out_specs=(vmem, vmem, vmem),
        compiler_params=pltpu.CompilerParams(vmem_limit_bytes=MAIN_VMEM),
    )(packed)


def solution(mesh):
    placed = (
        P(AXES, None, None, None),
        P(AXES, None),
        P(AXES),
        P(AXES),
        P(AXES),
        P(),
        P(AXES, None),
        P(AXES, None),
    )
    return jax.shard_map(
        on_device,
        mesh=mesh,
        in_specs=placed,
        out_specs=(P(None, AXES), P(None, AXES), P()),
        check_vma=False,
    )
```

profile of v0, /device:TPU:0, one launch (start us, length us, event | category | flops | bytes accessed | tf_op | source)
XLA Modules:
  0.0 41.0 jit_solution(10405846451410194602)
XLA Ops:
  1.3 38.4 %shard_map.103.packed = f32[21,128]{1,0:T(8,128)} custom-call(f32[1]{0:T(128)S(6)} %copy.11.beta_ref, s32[4]{0:T(128)} %count_ref.1, s32[4,24]{1,0:T(4,128)} %cols_ref.1, f32[4,128]{1,0:T(4,128)} %bitcast.3, f32[16,128]{1,0:T(8,128)} %bitcast.2, bf16[4,24,128,128]{3,2,1,0:T(8,128)(2,1)} %tiles_hbm.1, f32[512,128]{1,0:T(8,128)} %left_hbm.1, f32[2048,128]{1,0:T(8,128)} %right_hbm.1), custom_call_target="tpu_custom_call" | custom-call | tf_op jit(solution)/shard_map/pallas_call | solution.py:331
  39.7 1.3 %shard_map.104 = (f32[1,512]{1,0:T(1,128)}, f32[1,2048]{1,0:T(1,128)}, f32[2]{0:T(128)}) custom-call(f32[21,128]{1,0:T(8,128)} %shard_map.103.packed), custom_call_target="tpu_custom_call" | custom-call | tf_op jit(solution)/shard_map/pallas_call | solution.py:384
where the time goes:
time: 41.3 us; the launch traced here: 41 us
  Pallas kernels  39.7 us (96%)
  between operations  1.29 us (3%)
    pallas_call x1, Pallas kernels, on_device(): pl.pallas_call(functools.partial(steps_kernel, devices, planes, own_tiles...  38.4 us
    pallas_call x1, Pallas kernels, on_device(): pl.pallas_call(functools.partial(place_kernel, own_tiles, blocks), out_sh...  1.31 us

commit v1 on v0

v1 whole, which is shorter than its diff:
```python
import functools
import math

import jax
import jax.numpy as jnp
from jax import lax
from jax.experimental import pallas as pl
from jax.experimental.pallas import tpu as pltpu
from jax.sharding import PartitionSpec as P

AXES = ("blk", "plane")
LANES = 128
SUB = 8
NT_DIMS = (((1,), (1,)), ((), ()))
MAIN_VMEM = 67043328
MESH = pl.DeviceIdType.MESH
UNROLL_DEVICES = 32


def far_first(blks, planes):
    masks = [(b, p) for b in range(blks) for p in range(planes) if b or p]
    weight = lambda m: m[0] // 2 + m[0] % 2 + m[1] // 2 + 0.3 * (m[1] % 2)
    return sorted(masks, key=weight, reverse=True)


def flips(index, size):
    steps = []
    bit = 1
    while bit < size:
        steps.append(bit * (1 - 2 * lax.rem(index // bit, 2)))
        bit *= 2
    values = []
    for mask in range(size):
        value = index
        for k, step in enumerate(steps):
            if mask >> k & 1:
                value = value + step
        values.append(value)
    return values


def steps_kernel(
    blks,
    planes,
    own_tiles,
    left_scale,
    right_scale,
    beta_hbm,
    count_hbm,
    cols_hbm,
    u_hbm,
    v_hbm,
    tiles_hbm,
    left_hbm,
    right_hbm,
    out_ref,
    beta_s,
    count_s,
    cols_s,
    cols_v,
    u_scr,
    v_scr,
    tiles,
    left,
    right,
    left_t,
    right_t,
    v_send,
    v_all,
    v_table,
    cols_rows,
    put_hot,
    shift_scr,
    p_scr,
    contrib,
    gram_send,
    gram_recv,
    gram_sum,
    gram_all,
    gram_scr,
    dot_send,
    dot_recv,
    part_send,
    part_recv,
    copy_sem,
    send_sem,
    recv_sem,
):
    devices = blks * planes
    blocks, slots = cols_v.shape
    keep = left.shape[1]
    me_blk, me_plane = lax.axis_index("blk"), lax.axis_index("plane")
    me = me_blk * planes + me_plane
    chunks, rows = gram_send.shape[1:3]
    pad_tiles = v_send.shape[0]
    part_rows = part_send.shape[1]
    entries = contrib.shape[0]
    stride = entries // blocks
    two_power = blks & (blks - 1) == 0 and planes & (planes - 1) == 0
    unrolled = two_power and devices <= UNROLL_DEVICES
    if unrolled:
        blk_of, plane_of = flips(me_blk, blks), flips(me_plane, planes)
        order = far_first(blks, planes)

    def each_other(act):
        if unrolled:
            for b, p in order:
                act(blk_of[b] * planes + plane_of[p], (blk_of[b], plane_of[p]))
            return

        def body(step, carry):
            other = lax.rem(me + step, devices)
            act(other, (other // planes, lax.rem(other, planes)))
            return carry

        lax.fori_loop(1, devices, body, 0)

    barrier = pltpu.get_barrier_semaphore()
    each_other(
        lambda other, place: pl.semaphore_signal(
            barrier, inc=1, device_id=place, device_id_type=MESH
        )
    )

    pairs = (
        (v_hbm, v_scr),
        (cols_hbm, cols_v),
        (count_hbm, count_s),
        (cols_hbm, cols_s),
        (beta_hbm, beta_s),
        (u_hbm, u_scr),
        (left_hbm, left),
        (right_hbm, right),
        (tiles_hbm, tiles),
    )
    loads = [pltpu.make_async_copy(a, b, copy_sem.at[i]) for i, (a, b) in enumerate(pairs)]
    for load in loads:
        load.start()
    v_load, cols_load, count_load, index_load, beta_load, u_load, left_load, right_load, tiles_load = loads

    def send_all(phase, source, landing):
        each_other(
            lambda other, place: pltpu.make_async_remote_copy(
                src_ref=source(other),
                dst_ref=landing.at[me],
                send_sem=send_sem.at[phase],
                recv_sem=recv_sem.at[phase],
                device_id=place,
                device_id_type=MESH,
            ).start()
        )

    def wait_all(sem, phase, landing):
        most = landing.at[pl.ds(0, devices - 1)]
        pltpu.make_async_copy(most, most, sem.at[phase]).wait()

    eye = lax.broadcasted_iota(jnp.int32, (LANES, LANES), 0) == lax.broadcasted_iota(
        jnp.int32, (LANES, LANES), 1
    )

    def to_col(row):
        return jnp.sum(jnp.where(eye, row, 0.0), axis=1, keepdims=True)

    def to_row(col):
        return jnp.sum(jnp.where(eye, col, 0.0), axis=0, keepdims=True)

    def fold(block):
        return jnp.sum(block.reshape(LANES // SUB, SUB, LANES), axis=0)

    v_load.wait()
    rounded = v_scr[...]
    if pad_tiles > own_tiles:
        rounded = jnp.concatenate(
            [rounded, jnp.zeros((pad_tiles - own_tiles, LANES), jnp.float32)], axis=0
        )
    rounded = rounded.astype(jnp.bfloat16)
    v_send[...] = rounded
    v_all[me] = rounded
    v_table[devices * pad_tiles :, :] = jnp.zeros((SUB, LANES), jnp.float32)

    def start_gram(side, basis_t):
        whole = basis_t[...]
        high = whole.astype(jnp.bfloat16)
        rest = whole - high.astype(jnp.float32)
        mid = rest.astype(jnp.bfloat16)
        low = (rest - mid.astype(jnp.float32)).astype(jnp.bfloat16)

        def product(a, b):
            return lax.dot_general(a, b, NT_DIMS, preferred_element_type=jnp.float32)

        cross = product(high, mid) + product(high, low)
        gram = product(high, high) + (cross + cross.T + product(mid, mid))
        for c in range(chunks):
            gram_send[side, c] = gram[c * rows : (c + 1) * rows, :]
        gram_recv[side, me] = gram_send[side, lax.rem(me, chunks)]

    def send_gram(side, phase):
        send_all(
            phase, lambda other: gram_send.at[side, lax.rem(other, chunks)], gram_recv.at[side]
        )

    def share_gram(side, phase):
        wait_all(recv_sem, phase, gram_recv.at[side])
        mine = jnp.sum(gram_recv[side], axis=0)
        gram_sum[side] = mine
        gram_all[side, me] = mine
        send_all(phase + 1, lambda other: gram_sum.at[side], gram_all.at[side])

    def finish_gram(side, phase):
        wait_all(recv_sem, phase + 1, gram_all.at[side])
        for c in range(chunks):
            gram_scr[c * rows : (c + 1) * rows, :] = gram_all[side, c]
        return gram_scr[...]

    left_load.wait()
    for r in range(left.shape[0] // LANES):
        left_t[:, r * LANES : (r + 1) * LANES] = left[r * LANES : (r + 1) * LANES, :].T
    start_gram(0, left_t)

    pl.semaphore_wait(barrier, devices - 1)
    send_all(0, lambda other: v_send, v_all)
    send_gram(0, 1)

    cols_load.wait()
    count_load.wait()
    index_load.wait()
    beta_load.wait()
    u_load.wait()
    cols_rows[...] = jnp.full(cols_rows.shape, -1.0, jnp.float32)
    for r in range(blocks):
        row = cols_v[r : r + 1, :]
        alive = lax.broadcasted_iota(jnp.int32, (1, slots), 1) < count_s[r]
        cols_rows[r : r + 1, 0:slots] = jnp.where(alive, row, -1).astype(jnp.float32)
    lane = lax.broadcasted_iota(jnp.int32, (1, entries), 1)
    line = jnp.full((1, entries), -1.0, jnp.float32)
    for r in range(blocks):
        row = cols_rows[r : r + 1, :]
        if r:
            row = pltpu.roll(row, r * stride, 1)
        line = jnp.where((lane >= r * stride) & (lane < r * stride + slots), row, line)
    whole = line.astype(jnp.int32)
    put_row = jnp.where(whole < 0, -1, whole // own_tiles * part_rows + whole % own_tiles)
    hot = jnp.where(
        lax.broadcasted_iota(jnp.int32, (put_hot.shape[0], entries), 0) == put_row, 1.0, 0.0
    ).astype(jnp.bfloat16)
    put_hot[:, 0:entries] = hot
    put_hot[:, entries:] = hot
    contrib[...] = jnp.zeros_like(contrib)
    beta = beta_s[0]
    for r in range(blocks):
        shift_scr[r] = jnp.where(eye, -beta * u_scr[r : r + 1, :], 0.0)

    right_load.wait()
    for t in range(own_tiles):
        right_t[:, t * LANES : (t + 1) * LANES] = right[t * LANES : (t + 1) * LANES, :].T
    start_gram(1, right_t)
    tiles_load.wait()

    wait_all(recv_sem, 0, v_all)
    v_table[0 : devices * pad_tiles, :] = (
        v_all[...].reshape(devices * pad_tiles, LANES).astype(jnp.float32)
    )
    dots = jnp.zeros((SUB, LANES), jnp.float32)
    square = jnp.zeros((SUB, LANES), jnp.float32)
    for r in range(blocks):
        total = shift_scr[r]
        for s in range(slots):
            col = cols_s[r, s]
            if pad_tiles != own_tiles:
                col = col // own_tiles * pad_tiles + lax.rem(col, own_tiles)
            col = jnp.where(s < count_s[r], col, devices * pad_tiles)
            total = total + tiles[r, s].astype(jnp.float32) * v_table[pl.ds(col, 1), :]
        p_col = jnp.broadcast_to(jnp.sum(total, axis=1, keepdims=True), (LANES, LANES))
        p_scr[r] = p_col
        dots = dots + fold(left[r * LANES : (r + 1) * LANES, :] * p_col)
        square = square + fold(p_col * p_col)

    def start_dots(side, both):
        dot_send[side] = both
        dot_recv[side, me] = both
        send_all(3 + side, lambda other: dot_send.at[side], dot_recv.at[side])

    def finish_dots(side, phase):
        wait_all(recv_sem, 3 + side, dot_recv.at[side])
        both = jnp.sum(dot_recv[side], axis=0)
        first, square = both[0:1, :], both[1:2, :]
        gram = finish_gram(side, phase)
        twice = jnp.where(eye, 2.0, 0.0) - gram
        coef = jnp.sum(twice * first, axis=1, keepdims=True)
        coef_row = to_row(coef)
        spread = jnp.sum(gram * coef, axis=0, keepdims=True)
        change = jnp.sum(coef_row * (spread - 2.0 * first), axis=1, keepdims=True)
        return coef, coef_row, jnp.sqrt(square[0:1, 0:1] + change + 1e-06)

    start_dots(
        0,
        jnp.concatenate(
            [jnp.sum(dots, axis=0, keepdims=True), jnp.sum(square, axis=0, keepdims=True)], axis=0
        ),
    )
    share_gram(0, 1)
    send_gram(1, 6)

    coef, coef_row, alpha = finish_dots(0, 1)
    inverse = 1.0 / alpha

    for r in range(blocks):
        fix = jnp.sum(left[r * LANES : (r + 1) * LANES, :] * coef_row, axis=1, keepdims=True)
        p_scr[r] = (p_scr[r] - fix) * inverse

    for r in range(blocks):
        col = p_scr[r].astype(jnp.bfloat16).astype(jnp.float32)
        for g in range(0, slots, SUB):
            lines = [
                jnp.sum(fold(tiles[r, s].astype(jnp.float32) * col), axis=0, keepdims=True)
                for s in range(g, min(g + SUB, slots))
            ]
            contrib[r * stride + g : r * stride + g + len(lines), :] = jnp.concatenate(lines, axis=0)
    whole = contrib[...]
    high = whole.astype(jnp.bfloat16)
    low = (whole - high.astype(jnp.float32)).astype(jnp.bfloat16)
    spread = jnp.dot(
        put_hot[...], jnp.concatenate([high, low], axis=0), preferred_element_type=jnp.float32
    )
    part_send[...] = spread.reshape(devices, part_rows, LANES)
    part_recv[me] = part_send[me]
    send_all(5, lambda other: part_send.at[other], part_recv)
    share_gram(1, 6)
    for r in range(blocks):
        out_ref[own_tiles + r : own_tiles + r + 1, :] = to_row(p_scr[r]) * left_scale
    wait_all(recv_sem, 5, part_recv)
    own = jnp.sum(part_recv[...], axis=0)
    r_vec = own[0:own_tiles, :] - alpha * v_scr[...]

    total = jnp.zeros((keep, LANES), jnp.float32)
    for t in range(own_tiles):
        total = total + right_t[:, t * LANES : (t + 1) * LANES] * r_vec[t : t + 1, :]
    dots = to_row(jnp.sum(total, axis=1, keepdims=True))
    square = jnp.sum(r_vec * r_vec, keepdims=True)
    start_dots(1, jnp.concatenate([dots, jnp.broadcast_to(square, (1, LANES))], axis=0))
    coef, coef_row, beta_new = finish_dots(1, 6)
    place = lax.broadcasted_iota(jnp.int32, (1, LANES), 1)
    out_ref[own_tiles + blocks : own_tiles + blocks + 1, :] = jnp.where(
        place == 0, alpha, beta_new
    )
    inverse = right_scale / beta_new
    for t in range(own_tiles):
        fix = jnp.sum(right_t[:, t * LANES : (t + 1) * LANES] * coef, axis=0, keepdims=True)
        out_ref[t : t + 1, :] = (r_vec[t : t + 1, :] - fix) * inverse

    wait_all(send_sem, 0, v_all)
    for phase, side in ((1, 0), (6, 1)):
        wait_all(send_sem, phase, gram_recv.at[side])
        wait_all(send_sem, phase + 1, gram_all.at[side])
    wait_all(send_sem, 3, dot_recv.at[0])
    wait_all(send_sem, 4, dot_recv.at[1])
    wait_all(send_sem, 5, part_recv)


def place_kernel(own_tiles, blocks, packed, out_left, out_right, out_coef):
    for r in range(blocks):
        out_left[:, r * LANES : (r + 1) * LANES] = packed[own_tiles + r : own_tiles + r + 1, :]
    for t in range(own_tiles):
        out_right[:, t * LANES : (t + 1) * LANES] = packed[t : t + 1, :]
    out_coef[...] = packed[own_tiles + blocks, 0:2]


def on_device(tiles, tile_cols, tile_count, u_start, v_start, beta_start, left_basis, right_basis):
    blks, planes = lax.axis_size("blk"), lax.axis_size("plane")
    devices = blks * planes
    blocks, slots = tile_cols.shape
    own_tiles = v_start.shape[0] // LANES
    left_rows, keep = left_basis.shape
    right_rows = right_basis.shape[0]
    pad_tiles = -(-own_tiles // 16) * 16
    part_rows = -(-own_tiles // 8) * 8
    rows = max(4, keep // devices)
    chunks = keep // rows
    stride = -(-slots // 8) * 8
    while (blocks * stride) % LANES:
        stride += 8
    entries = blocks * stride
    f32, bf16, i32 = jnp.float32, jnp.bfloat16, jnp.int32
    vmem = pl.BlockSpec(memory_space=pltpu.VMEM)
    hbm = pl.BlockSpec(memory_space=pl.ANY)
    packed = pl.pallas_call(
        functools.partial(
            steps_kernel,
            blks,
            planes,
            own_tiles,
            math.sqrt(left_rows * devices),
            math.sqrt(right_rows * devices),
        ),
        out_shape=jax.ShapeDtypeStruct((own_tiles + blocks + 1, LANES), f32),
        in_specs=[hbm] * 8,
        out_specs=vmem,
        scratch_shapes=[
            pltpu.SMEM((1,), f32),
            pltpu.SMEM((blocks,), i32),
            pltpu.SMEM((blocks, slots), i32),
            pltpu.VMEM((blocks, slots), i32),
            pltpu.VMEM((blocks, LANES), f32),
            pltpu.VMEM((own_tiles, LANES), f32),
            pltpu.VMEM(tiles.shape, bf16),
            pltpu.VMEM(left_basis.shape, f32),
            pltpu.VMEM(right_basis.shape, f32),
            pltpu.VMEM((keep, left_rows), f32),
            pltpu.VMEM((keep, right_rows), f32),
            pltpu.VMEM((pad_tiles, LANES), bf16),
            pltpu.VMEM((devices, pad_tiles, LANES), bf16),
            pltpu.VMEM((devices * pad_tiles + SUB, LANES), f32),
            pltpu.VMEM((-(-blocks // 8) * 8, entries), f32),
            pltpu.VMEM((devices * part_rows, 2 * entries), bf16),
            pltpu.VMEM((blocks, LANES, LANES), f32),
            pltpu.VMEM((blocks, LANES, LANES), f32),
            pltpu.VMEM((entries, LANES), f32),
            pltpu.VMEM((2, chunks, rows, keep), f32),
            pltpu.VMEM((2, devices, rows, keep), f32),
            pltpu.VMEM((2, rows, keep), f32),
            pltpu.VMEM((2, devices, rows, keep), f32),
            pltpu.VMEM((keep, keep), f32),
            pltpu.VMEM((2, 2, keep), f32),
            pltpu.VMEM((2, devices, 2, keep), f32),
            pltpu.VMEM((devices, part_rows, LANES), f32),
            pltpu.VMEM((devices, part_rows, LANES), f32),
            pltpu.SemaphoreType.DMA((9,)),
            pltpu.SemaphoreType.DMA((8,)),
            pltpu.SemaphoreType.DMA((8,)),
        ],
        compiler_params=pltpu.CompilerParams(
            collective_id=0, has_side_effects=True, vmem_limit_bytes=MAIN_VMEM
        ),
    )(
        beta_start,
        tile_count,
        tile_cols,
        u_start.reshape(blocks, LANES),
        v_start.reshape(own_tiles, LANES),
        tiles,
        left_basis,
        right_basis,
    )
    return pl.pallas_call(
        functools.partial(place_kernel, own_tiles, blocks),
        out_shape=(
            jax.ShapeDtypeStruct((1, left_rows), f32),
            jax.ShapeDtypeStruct((1, right_rows), f32),
            jax.ShapeDtypeStruct((2,), f32),
        ),
        in_specs=[vmem],
        out_specs=(vmem, vmem, vmem),
        compiler_params=pltpu.CompilerParams(vmem_limit_bytes=MAIN_VMEM),
    )(packed)


def solution(mesh):
    placed = (
        P(AXES, None, None, None),
        P(AXES, None),
        P(AXES),
        P(AXES),
        P(AXES),
        P(),
        P(AXES, None),
        P(AXES, None),
    )
    return jax.shard_map(
        on_device,
        mesh=mesh,
        in_specs=placed,
        out_specs=(P(None, AXES), P(None, AXES), P()),
        check_vma=False,
    )
```

time: 41.3 us -> 37.2 us (0.901)
  Pallas kernels: 39.7 us -> 35.6 us
    pallas_call x1, Pallas kernels: 38.4 us -> 34.3 us  [on_device(): pl.pallas_call(functools.partial(steps_kernel, blks, planes, own_tiles, m...]
where the time goes in v1:
time: 37.2 us; the launch traced here: 36.9 us
  Pallas kernels  35.6 us (96%)
  between operations  1.29 us (3%)
    pallas_call x1, Pallas kernels, on_device(): pl.pallas_call(functools.partial(steps_kernel, blks, planes, own_tiles, m...  34.3 us
    pallas_call x1, Pallas kernels, on_device(): pl.pallas_call(functools.partial(place_kernel, own_tiles, blocks), out_sh...  1.31 us

profile of v1, /device:TPU:0, one launch (start us, length us, event | category | flops | bytes accessed | tf_op | source)
XLA Modules:
  0.0 36.9 jit_solution(3128145841421263368)
XLA Ops:
  1.3 34.3 %shard_map.103.packed = f32[21,128]{1,0:T(8,128)} custom-call(f32[1]{0:T(128)S(6)} %copy.11.beta_hbm, s32[4]{0:T(128)} %count_hbm.1, s32[4,24]{1,0:T(4,128)} %cols_hbm.1, f32[4,128]{1,0:T(4,128)} %bitcast.3, f32[16,128]{1,0:T(8,128)} %bitcast.2, bf16[4,24,128,128]{3,2,1,0:T(8,128)(2,1)} %tiles_hbm.1, f32[512,128]{1,0:T(8,128)} %left_hbm.1, f32[2048,128]{1,0:T(8,128)} %right_hbm.1), custom_call_target="tpu_custom_call" | custom-call | tf_op jit(solution)/shard_map/pallas_call | solution.py:386
  35.6 1.3 %shard_map.104 = (f32[1,512]{1,0:T(1,128)}, f32[1,2048]{1,0:T(1,128)}, f32[2]{0:T(128)}) custom-call(f32[21,128]{1,0:T(8,128)} %shard_map.103.packed), custom_call_target="tpu_custom_call" | custom-call | tf_op jit(solution)/shard_map/pallas_call | solution.py:444

commit v2 on v1

--- a/solution.py
+++ b/solution.py
@@ -93,7 +93,8 @@
     me = me_blk * planes + me_plane
     chunks, rows = gram_send.shape[1:3]
     pad_tiles = v_send.shape[0]
-    part_rows = part_send.shape[1]
+    words = part_send.shape[1] - 1
+    part_rows = 2 * words
     entries = contrib.shape[0]
     stride = entries // blocks
     two_power = blks & (blks - 1) == 0 and planes & (planes - 1) == 0
@@ -322,14 +323,26 @@
     spread = jnp.dot(
         put_hot[...], jnp.concatenate([high, low], axis=0), preferred_element_type=jnp.float32
     )
-    part_send[...] = spread.reshape(devices, part_rows, LANES)
+    parts = spread.reshape(devices, part_rows, LANES)
+    top = jnp.maximum(jnp.max(jnp.abs(parts), axis=1, keepdims=True), 1e-30)
+    power = jnp.floor(jnp.log2(top)) - 14.0
+    whole = jnp.minimum(jnp.round(parts * jnp.exp2(-power)), 32767.0).astype(jnp.int32)
+    part_send[:, 0:words, :] = lax.shift_left(whole[:, 0:words, :], 16) | (
+        whole[:, words:, :] & 0xFFFF
+    )
+    part_send[:, words:, :] = power.astype(jnp.int32)
     part_recv[me] = part_send[me]
     send_all(5, lambda other: part_send.at[other], part_recv)
     share_gram(1, 6)
     for r in range(blocks):
         out_ref[own_tiles + r : own_tiles + r + 1, :] = to_row(p_scr[r]) * left_scale
     wait_all(recv_sem, 5, part_recv)
-    own = jnp.sum(part_recv[...], axis=0)
+    unit = jnp.exp2(part_recv[:, words:, :].astype(jnp.float32))
+    word = part_recv[:, 0:words, :]
+    halves = (lax.shift_right_arithmetic(word, 16), lax.shift_right_arithmetic(lax.shift_left(word, 16), 16))
+    own = jnp.concatenate(
+        [jnp.sum(half.astype(jnp.float32) * unit, axis=0) for half in halves], axis=0
+    )
     r_vec = own[0:own_tiles, :] - alpha * v_scr[...]
 
     total = jnp.zeros((keep, LANES), jnp.float32)
@@ -373,7 +386,7 @@
     left_rows, keep = left_basis.shape
     right_rows = right_basis.shape[0]
     pad_tiles = -(-own_tiles // 16) * 16
-    part_rows = -(-own_tiles // 8) * 8
+    part_rows = -(-own_tiles // 16) * 16
     rows = max(4, keep // devices)
     chunks = keep // rows
     stride = -(-slots // 8) * 8
@@ -392,7 +405,7 @@
             math.sqrt(left_rows * devices),
             math.sqrt(right_rows * devices),
         ),
-        out_shape=jax.ShapeDtypeStruct((own_tiles + blocks + 1, LANES), f32),
+        out_shape=pltpu.VMEM((own_tiles + blocks + 1, LANES), f32),
         in_specs=[hbm] * 8,
         out_specs=vmem,
         scratch_shapes=[
@@ -422,14 +435,14 @@
             pltpu.VMEM((keep, keep), f32),
             pltpu.VMEM((2, 2, keep), f32),
             pltpu.VMEM((2, devices, 2, keep), f32),
-            pltpu.VMEM((devices, part_rows, LANES), f32),
-            pltpu.VMEM((devices, part_rows, LANES), f32),
+            pltpu.VMEM((devices, part_rows // 2 + 1, LANES), i32),
+            pltpu.VMEM((devices, part_rows // 2 + 1, LANES), i32),
             pltpu.SemaphoreType.DMA((9,)),
             pltpu.SemaphoreType.DMA((8,)),
             pltpu.SemaphoreType.DMA((8,)),
         ],
         compiler_params=pltpu.CompilerParams(
-            collective_id=0, has_side_effects=True, vmem_limit_bytes=MAIN_VMEM
+            collective_id=0, has_side_effects=True, vmem_limit_bytes=MAIN_VMEM - 512 * (-(-(own_tiles + blocks + 1) // SUB) * SUB)
         ),
     )(
         beta_start,
@@ -450,7 +463,7 @@
         ),
         in_specs=[vmem],
         out_specs=(vmem, vmem, vmem),
-        compiler_params=pltpu.CompilerParams(vmem_limit_bytes=MAIN_VMEM),
+        compiler_params=pltpu.CompilerParams(vmem_limit_bytes=1048576),
     )(packed)
 
 

time: 37.2 us -> 33.4 us (0.90)
  Pallas kernels: 35.6 us -> 31.9 us
    pallas_call x1, Pallas kernels: 34.3 us -> 31.3 us  [on_device(): pl.pallas_call(functools.partial(steps_kernel, blks, planes, own_tiles, m...]
    pallas_call x1, Pallas kernels: 1.31 us -> 0.61 us  [on_device(): pl.pallas_call(functools.partial(place_kernel, own_tiles, blocks), out_sh...]
where the time goes in v2:
time: 33.4 us; the launch traced here: 33.2 us
  Pallas kernels  31.9 us (96%)
  between operations  1.29 us (4%)
    pallas_call x1, Pallas kernels, on_device(): pl.pallas_call(functools.partial(steps_kernel, blks, planes, own_tiles, m...  31.3 us

profile of v2, /device:TPU:0, one launch (start us, length us, event | category | flops | bytes accessed | tf_op | source)
XLA Modules:
  0.0 33.2 jit_solution(14623275242760482371)
XLA Ops:
  1.3 31.3 %shard_map.103.packed = f32[21,128]{1,0:T(8,128)S(1)} custom-call(f32[1]{0:T(128)S(6)} %copy.11.beta_hbm, s32[4]{0:T(128)} %count_hbm.1, s32[4,24]{1,0:T(4,128)} %cols_hbm.1, f32[4,128]{1,0:T(4,128)} %bitcast.3, f32[16,128]{1,0:T(8,128)} %bitcast.2, bf16[4,24,128,128]{3,2,1,0:T(8,128)(2,1)} %tiles_hbm.1, f32[512,128]{1,0:T(8,128)} %left_hbm.1, ...), custom_call_target="tpu_custom_call" | custom-call | tf_op jit(solution)/shard_map/pallas_call | solution.py:399
  32.6 0.6 %shard_map.104 = (f32[1,512]{1,0:T(1,128)}, f32[1,2048]{1,0:T(1,128)}, f32[2]{0:T(128)}) custom-call(f32[21,128]{1,0:T(8,128)S(1)} %shard_map.103.packed), custom_call_target="tpu_custom_call" | custom-call | tf_op jit(solution)/shard_map/pallas_call | solution.py:457

commit v3 on v2

--- a/solution.py
+++ b/solution.py
@@ -11,6 +11,7 @@
 AXES = ("blk", "plane")
 LANES = 128
 SUB = 8
+ON_MXU = (2, 5, 7)
 NT_DIMS = (((1,), (1,)), ((), ()))
 MAIN_VMEM = 67043328
 MESH = pl.DeviceIdType.MESH
@@ -78,6 +79,7 @@
     gram_sum,
     gram_all,
     gram_scr,
+    diagonal,
     dot_send,
     dot_recv,
     part_send,
@@ -159,6 +161,10 @@
         jnp.int32, (LANES, LANES), 1
     )
 
+    half = keep // 2
+    half_row = lax.broadcasted_iota(jnp.int32, (half, keep), 0)
+    half_lane = lax.broadcasted_iota(jnp.int32, (half, keep), 1)
+
     def to_col(row):
         return jnp.sum(jnp.where(eye, row, 0.0), axis=1, keepdims=True)
 
@@ -191,8 +197,13 @@
 
         cross = product(high, mid) + product(high, low)
         gram = product(high, high) + (cross + cross.T + product(mid, mid))
+        top, low = gram[0:half, :], pltpu.roll(gram[half:, :], half, 1)
+        folded = jnp.where(half_lane >= half_row, top, low)
         for c in range(chunks):
-            gram_send[side, c] = gram[c * rows : (c + 1) * rows, :]
+            gram_send[side, c] = folded[c * rows : (c + 1) * rows, :]
+        diagonal[side] = jnp.sum(
+            jnp.where(half_lane == half_row + half, gram[half:, :], 0.0), axis=0, keepdims=True
+        )
         gram_recv[side, me] = gram_send[side, lax.rem(me, chunks)]
 
     def send_gram(side, phase):
@@ -211,7 +222,16 @@
         wait_all(recv_sem, phase + 1, gram_all.at[side])
         for c in range(chunks):
             gram_scr[c * rows : (c + 1) * rows, :] = gram_all[side, c]
-        return gram_scr[...]
+        folded = gram_scr[...]
+        strict = jnp.concatenate(
+            [
+                jnp.where(half_lane > half_row, folded, 0.0),
+                pltpu.roll(jnp.where(half_lane < half_row, folded, 0.0), half, 1),
+            ],
+            axis=0,
+        )
+        main = jnp.sum(jnp.where(half_lane == half_row, folded, 0.0), axis=0, keepdims=True)
+        return strict + strict.T + jnp.where(eye, main, 0.0)
 
     left_load.wait()
     for r in range(left.shape[0] // LANES):
@@ -264,6 +284,8 @@
     dots = jnp.zeros((SUB, LANES), jnp.float32)
     square = jnp.zeros((SUB, LANES), jnp.float32)
     for r in range(blocks):
+        if r == blocks - 1:
+            share_gram(0, 1)
         total = shift_scr[r]
         for s in range(slots):
             col = cols_s[r, s]
@@ -276,30 +298,30 @@
         dots = dots + fold(left[r * LANES : (r + 1) * LANES, :] * p_col)
         square = square + fold(p_col * p_col)
 
-    def start_dots(side, both):
+    def start_dots(side, dots, square):
+        lane = lax.broadcasted_iota(jnp.int32, (1, keep), 1)
+        both = jnp.concatenate([dots, jnp.where(lane >= half, diagonal[side], square)], axis=0)
         dot_send[side] = both
         dot_recv[side, me] = both
         send_all(3 + side, lambda other: dot_send.at[side], dot_recv.at[side])
 
     def finish_dots(side, phase):
+        gram = finish_gram(side, phase)
         wait_all(recv_sem, 3 + side, dot_recv.at[side])
         both = jnp.sum(dot_recv[side], axis=0)
-        first, square = both[0:1, :], both[1:2, :]
-        gram = finish_gram(side, phase)
+        first, square = both[0:1, :], both[1:2, 0:1]
+        lane = lax.broadcasted_iota(jnp.int32, (1, keep), 1)
+        gram = gram + jnp.where(eye & (lane >= half), both[1:2, :], 0.0)
         twice = jnp.where(eye, 2.0, 0.0) - gram
         coef = jnp.sum(twice * first, axis=1, keepdims=True)
         coef_row = to_row(coef)
         spread = jnp.sum(gram * coef, axis=0, keepdims=True)
         change = jnp.sum(coef_row * (spread - 2.0 * first), axis=1, keepdims=True)
-        return coef, coef_row, jnp.sqrt(square[0:1, 0:1] + change + 1e-06)
+        return coef, coef_row, jnp.sqrt(square + change + 1e-06)
 
     start_dots(
-        0,
-        jnp.concatenate(
-            [jnp.sum(dots, axis=0, keepdims=True), jnp.sum(square, axis=0, keepdims=True)], axis=0
-        ),
-    )
-    share_gram(0, 1)
+        0, jnp.sum(dots, axis=0, keepdims=True), jnp.sum(square, axis=0, keepdims=True)
+    )
     send_gram(1, 6)
 
     coef, coef_row, alpha = finish_dots(0, 1)
@@ -309,14 +331,20 @@
         fix = jnp.sum(left[r * LANES : (r + 1) * LANES, :] * coef_row, axis=1, keepdims=True)
         p_scr[r] = (p_scr[r] - fix) * inverse
 
-    for r in range(blocks):
-        col = p_scr[r].astype(jnp.bfloat16).astype(jnp.float32)
+    spot = lax.broadcasted_iota(jnp.int32, (SUB, LANES), 0)
+    for r in range(blocks):
+        rounded = p_scr[r].astype(jnp.bfloat16)
+        col = rounded.astype(jnp.float32)
+        row = jnp.broadcast_to(to_row(col), (2 * SUB, LANES)).astype(jnp.bfloat16)
         for g in range(0, slots, SUB):
-            lines = [
-                jnp.sum(fold(tiles[r, s].astype(jnp.float32) * col), axis=0, keepdims=True)
-                for s in range(g, min(g + SUB, slots))
-            ]
-            contrib[r * stride + g : r * stride + g + len(lines), :] = jnp.concatenate(lines, axis=0)
+            lines = jnp.zeros((SUB, LANES), jnp.float32)
+            for s in range(g, min(g + SUB, slots)):
+                if s % SUB in ON_MXU:
+                    line = jnp.dot(row, tiles[r, s], preferred_element_type=jnp.float32)[0:SUB, :]
+                else:
+                    line = jnp.sum(fold(tiles[r, s].astype(jnp.float32) * col), axis=0, keepdims=True)
+                lines = jnp.where(spot == s - g, line, lines)
+            contrib[r * stride + g : r * stride + g + SUB, :] = lines
     whole = contrib[...]
     high = whole.astype(jnp.bfloat16)
     low = (whole - high.astype(jnp.float32)).astype(jnp.bfloat16)
@@ -333,10 +361,10 @@
     part_send[:, words:, :] = power.astype(jnp.int32)
     part_recv[me] = part_send[me]
     send_all(5, lambda other: part_send.at[other], part_recv)
-    share_gram(1, 6)
     for r in range(blocks):
         out_ref[own_tiles + r : own_tiles + r + 1, :] = to_row(p_scr[r]) * left_scale
     wait_all(recv_sem, 5, part_recv)
+    share_gram(1, 6)
     unit = jnp.exp2(part_recv[:, words:, :].astype(jnp.float32))
     word = part_recv[:, 0:words, :]
     halves = (lax.shift_right_arithmetic(word, 16), lax.shift_right_arithmetic(lax.shift_left(word, 16), 16))
@@ -350,7 +378,7 @@
         total = total + right_t[:, t * LANES : (t + 1) * LANES] * r_vec[t : t + 1, :]
     dots = to_row(jnp.sum(total, axis=1, keepdims=True))
     square = jnp.sum(r_vec * r_vec, keepdims=True)
-    start_dots(1, jnp.concatenate([dots, jnp.broadcast_to(square, (1, LANES))], axis=0))
+    start_dots(1, dots, jnp.broadcast_to(square, (1, LANES)))
     coef, coef_row, beta_new = finish_dots(1, 6)
     place = lax.broadcasted_iota(jnp.int32, (1, LANES), 1)
     out_ref[own_tiles + blocks : own_tiles + blocks + 1, :] = jnp.where(
@@ -387,8 +415,8 @@
     right_rows = right_basis.shape[0]
     pad_tiles = -(-own_tiles // 16) * 16
     part_rows = -(-own_tiles // 16) * 16
-    rows = max(4, keep // devices)
-    chunks = keep // rows
+    rows = max(2, keep // 2 // devices)
+    chunks = keep // 2 // rows
     stride = -(-slots // 8) * 8
     while (blocks * stride) % LANES:
         stride += 8
@@ -432,7 +460,8 @@
             pltpu.VMEM((2, devices, rows, keep), f32),
             pltpu.VMEM((2, rows, keep), f32),
             pltpu.VMEM((2, devices, rows, keep), f32),
-            pltpu.VMEM((keep, keep), f32),
+            pltpu.VMEM((keep // 2, keep), f32),
+            pltpu.VMEM((2, 1, keep), f32),
             pltpu.VMEM((2, 2, keep), f32),
             pltpu.VMEM((2, devices, 2, keep), f32),
             pltpu.VMEM((devices, part_rows // 2 + 1, LANES), i32),

time: 33.4 us -> 31.4 us (0.940)
  Pallas kernels: 31.9 us -> 29.9 us
    pallas_call x1, Pallas kernels: 31.3 us -> 29.3 us  [on_device(): pl.pallas_call(functools.partial(steps_kernel, blks, planes, own_tiles, m...]
where the time goes in v3:
time: 31.4 us; the launch traced here: 31.2 us
  Pallas kernels  29.9 us (95%)
  between operations  1.29 us (4%)
    pallas_call x1, Pallas kernels, on_device(): pl.pallas_call(functools.partial(steps_kernel, blks, planes, own_tiles, m...  29.3 us

profile of v3, /device:TPU:0, one launch (start us, length us, event | category | flops | bytes accessed | tf_op | source)
XLA Modules:
  0.0 31.2 jit_solution(14680409043640332750)
XLA Ops:
  1.3 29.3 %shard_map.103.packed = f32[21,128]{1,0:T(8,128)S(1)} custom-call(f32[1]{0:T(128)S(6)} %copy.11.beta_hbm, s32[4]{0:T(128)} %count_hbm.1, s32[4,24]{1,0:T(4,128)} %cols_hbm.1, f32[4,128]{1,0:T(4,128)} %bitcast.3, f32[16,128]{1,0:T(8,128)} %bitcast.2, bf16[4,24,128,128]{3,2,1,0:T(8,128)(2,1)} %tiles_hbm.1, f32[512,128]{1,0:T(8,128)} %left_hbm.1, ...), custom_call_target="tpu_custom_call" | custom-call | tf_op jit(solution)/shard_map/pallas_call | solution.py:427
  30.6 0.6 %shard_map.104 = (f32[1,512]{1,0:T(1,128)}, f32[1,2048]{1,0:T(1,128)}, f32[2]{0:T(128)}) custom-call(f32[21,128]{1,0:T(8,128)S(1)} %shard_map.103.packed), custom_call_target="tpu_custom_call" | custom-call | tf_op jit(solution)/shard_map/pallas_call | solution.py:486

commit v4 on v3

--- a/solution.py
+++ b/solution.py
@@ -118,6 +118,12 @@
 
         lax.fori_loop(1, devices, body, 0)
 
+    owners = gram_all.shape[1]
+    owner_blks = owners // planes
+    first_owner = (blks - owner_blks) // 2
+    owner = (me_blk >= first_owner) & (me_blk < first_owner + owner_blks)
+    my_part = me - first_owner * planes
+
     barrier = pltpu.get_barrier_semaphore()
     each_other(
         lambda other, place: pl.semaphore_signal(
@@ -141,17 +147,18 @@
         load.start()
     v_load, cols_load, count_load, index_load, beta_load, u_load, left_load, right_load, tiles_load = loads
 
+    def send_one(phase, source, landing, place):
+        pltpu.make_async_remote_copy(
+            src_ref=source,
+            dst_ref=landing,
+            send_sem=send_sem.at[phase],
+            recv_sem=recv_sem.at[phase],
+            device_id=place,
+            device_id_type=MESH,
+        ).start()
+
     def send_all(phase, source, landing):
-        each_other(
-            lambda other, place: pltpu.make_async_remote_copy(
-                src_ref=source(other),
-                dst_ref=landing.at[me],
-                send_sem=send_sem.at[phase],
-                recv_sem=recv_sem.at[phase],
-                device_id=place,
-                device_id_type=MESH,
-            ).start()
-        )
+        each_other(lambda other, place: send_one(phase, source(other), landing.at[me], place))
 
     def wait_all(sem, phase, landing):
         most = landing.at[pl.ds(0, devices - 1)]
@@ -204,22 +211,58 @@
         diagonal[side] = jnp.sum(
             jnp.where(half_lane == half_row + half, gram[half:, :], 0.0), axis=0, keepdims=True
         )
-        gram_recv[side, me] = gram_send[side, lax.rem(me, chunks)]
+        gram_recv[side, me] = gram_send[side, lax.rem(my_part + owners, chunks)]
 
     def send_gram(side, phase):
-        send_all(
-            phase, lambda other: gram_send.at[side, lax.rem(other, chunks)], gram_recv.at[side]
-        )
+        def send(part, place):
+            send_one(
+                phase,
+                gram_send.at[side, lax.rem(part, chunks)],
+                gram_recv.at[side, me],
+                place,
+            )
+
+        if unrolled:
+            near = flips(lax.rem(me_blk, owner_blks), owner_blks)
+            for k in reversed(range(owner_blks)):
+                for p in reversed(range(planes)):
+                    part = near[k] * planes + plane_of[p]
+                    place = (first_owner + near[k], plane_of[p])
+                    if k == first_owner and p == 0:
+                        pl.when(jnp.logical_not(owner))(functools.partial(send, part, place))
+                    else:
+                        send(part, place)
+            return
+
+        def body(step, carry):
+            part = lax.rem(me + step, owners)
+            place = (first_owner + part // planes, lax.rem(part, planes))
+            pl.when(part != my_part)(functools.partial(send, part, place))
+            return carry
+
+        lax.fori_loop(0, owners, body, 0)
 
     def share_gram(side, phase):
-        wait_all(recv_sem, phase, gram_recv.at[side])
-        mine = jnp.sum(gram_recv[side], axis=0)
-        gram_sum[side] = mine
-        gram_all[side, me] = mine
-        send_all(phase + 1, lambda other: gram_sum.at[side], gram_all.at[side])
+        @pl.when(owner)
+        def _():
+            wait_all(recv_sem, phase, gram_recv.at[side])
+            mine = jnp.sum(gram_recv[side], axis=0)
+            gram_sum[side] = mine
+            gram_all[side, jnp.clip(my_part, 0, owners - 1)] = mine
+            each_other(
+                lambda other, place: send_one(
+                    phase + 1, gram_sum.at[side], gram_all.at[side, my_part], place
+                )
+            )
+
+    def wait_owned(sem, phase, landing):
+        for mine, size in ((owner, owners - 1), (jnp.logical_not(owner), owners)):
+            if size:
+                most = landing.at[pl.ds(0, size)]
+                pl.when(mine)(pltpu.make_async_copy(most, most, sem.at[phase]).wait)
 
     def finish_gram(side, phase):
-        wait_all(recv_sem, phase + 1, gram_all.at[side])
+        wait_owned(recv_sem, phase + 1, gram_all.at[side])
         for c in range(chunks):
             gram_scr[c * rows : (c + 1) * rows, :] = gram_all[side, c]
         folded = gram_scr[...]
@@ -391,8 +434,8 @@
 
     wait_all(send_sem, 0, v_all)
     for phase, side in ((1, 0), (6, 1)):
-        wait_all(send_sem, phase, gram_recv.at[side])
-        wait_all(send_sem, phase + 1, gram_all.at[side])
+        wait_owned(send_sem, phase, gram_all.at[side])
+        pl.when(owner)(functools.partial(wait_all, send_sem, phase + 1, gram_recv.at[side]))
     wait_all(send_sem, 3, dot_recv.at[0])
     wait_all(send_sem, 4, dot_recv.at[1])
     wait_all(send_sem, 5, part_recv)
@@ -415,7 +458,8 @@
     right_rows = right_basis.shape[0]
     pad_tiles = -(-own_tiles // 16) * 16
     part_rows = -(-own_tiles // 16) * 16
-    rows = max(2, keep // 2 // devices)
+    owners = (blks // 2 if blks % 4 == 0 else blks) * planes
+    rows = max(2, keep // 2 // owners)
     chunks = keep // 2 // rows
     stride = -(-slots // 8) * 8
     while (blocks * stride) % LANES:
@@ -459,7 +503,7 @@
             pltpu.VMEM((2, chunks, rows, keep), f32),
             pltpu.VMEM((2, devices, rows, keep), f32),
             pltpu.VMEM((2, rows, keep), f32),
-            pltpu.VMEM((2, devices, rows, keep), f32),
+            pltpu.VMEM((2, owners, rows, keep), f32),
             pltpu.VMEM((keep // 2, keep), f32),
             pltpu.VMEM((2, 1, keep), f32),
             pltpu.VMEM((2, 2, keep), f32),

time: 31.4 us -> 31.2 us (level)
  no operation moved by 1% of the time
where the time goes in v4:
time: 31.2 us; the launch traced here: 31 us
  Pallas kernels  29.7 us (95%)
  between operations  1.29 us (4%)
    pallas_call x1, Pallas kernels, on_device(): pl.pallas_call(functools.partial(steps_kernel, blks, planes, own_tiles, m...  29.1 us

profile of v4, /device:TPU:0, one launch (start us, length us, event | category | flops | bytes accessed | tf_op | source)
XLA Modules:
  0.0 31.0 jit_solution(125303599571168570)
XLA Ops:
  1.3 29.1 %shard_map.103.packed = f32[21,128]{1,0:T(8,128)S(1)} custom-call(f32[1]{0:T(128)S(6)} %copy.11.beta_hbm, s32[4]{0:T(128)} %count_hbm.1, s32[4,24]{1,0:T(4,128)} %cols_hbm.1, f32[4,128]{1,0:T(4,128)} %bitcast.3, f32[16,128]{1,0:T(8,128)} %bitcast.2, bf16[4,24,128,128]{3,2,1,0:T(8,128)(2,1)} %tiles_hbm.1, f32[512,128]{1,0:T(8,128)} %left_hbm.1, ...), custom_call_target="tpu_custom_call" | custom-call | tf_op jit(solution)/shard_map/pallas_call | solution.py:471
  30.4 0.6 %shard_map.104 = (f32[1,512]{1,0:T(1,128)}, f32[1,2048]{1,0:T(1,128)}, f32[2]{0:T(128)}) custom-call(f32[21,128]{1,0:T(8,128)S(1)} %shard_map.103.packed), custom_call_target="tpu_custom_call" | custom-call | tf_op jit(solution)/shard_map/pallas_call | solution.py:530

commit v5 on v4

--- a/solution.py
+++ b/solution.py
@@ -11,16 +11,17 @@
 AXES = ("blk", "plane")
 LANES = 128
 SUB = 8
-ON_MXU = (2, 5, 7)
+ON_MXU = (0, 1, 2)
 NT_DIMS = (((1,), (1,)), ((), ()))
 MAIN_VMEM = 67043328
 MESH = pl.DeviceIdType.MESH
+RECV = (0, 1, 2, 3, 3, 0, 4, 2)
 UNROLL_DEVICES = 32
 
 
 def far_first(blks, planes):
     masks = [(b, p) for b in range(blks) for p in range(planes) if b or p]
-    weight = lambda m: m[0] // 2 + m[0] % 2 + m[1] // 2 + 0.3 * (m[1] % 2)
+    weight = lambda m: 0.6 * (m[0] // 2) + m[0] % 2 + m[1] // 2 - 0.3 * (m[1] % 2)
     return sorted(masks, key=weight, reverse=True)
 
 
@@ -84,6 +85,7 @@
     dot_recv,
     part_send,
     part_recv,
+    sent,
     copy_sem,
     send_sem,
     recv_sem,
@@ -151,8 +153,8 @@
         pltpu.make_async_remote_copy(
             src_ref=source,
             dst_ref=landing,
-            send_sem=send_sem.at[phase],
-            recv_sem=recv_sem.at[phase],
+            send_sem=send_sem.at[0],
+            recv_sem=recv_sem.at[RECV[phase]],
             device_id=place,
             device_id_type=MESH,
         ).start()
@@ -160,9 +162,9 @@
     def send_all(phase, source, landing):
         each_other(lambda other, place: send_one(phase, source(other), landing.at[me], place))
 
-    def wait_all(sem, phase, landing):
+    def wait_all(phase, landing):
         most = landing.at[pl.ds(0, devices - 1)]
-        pltpu.make_async_copy(most, most, sem.at[phase]).wait()
+        pltpu.make_async_copy(most, most, recv_sem.at[RECV[phase]]).wait()
 
     eye = lax.broadcasted_iota(jnp.int32, (LANES, LANES), 0) == lax.broadcasted_iota(
         jnp.int32, (LANES, LANES), 1
@@ -245,7 +247,7 @@
     def share_gram(side, phase):
         @pl.when(owner)
         def _():
-            wait_all(recv_sem, phase, gram_recv.at[side])
+            wait_all(phase, gram_recv.at[side])
             mine = jnp.sum(gram_recv[side], axis=0)
             gram_sum[side] = mine
             gram_all[side, jnp.clip(my_part, 0, owners - 1)] = mine
@@ -255,14 +257,14 @@
                 )
             )
 
-    def wait_owned(sem, phase, landing):
+    def wait_owned(phase, landing):
         for mine, size in ((owner, owners - 1), (jnp.logical_not(owner), owners)):
             if size:
                 most = landing.at[pl.ds(0, size)]
-                pl.when(mine)(pltpu.make_async_copy(most, most, sem.at[phase]).wait)
+                pl.when(mine)(pltpu.make_async_copy(most, most, recv_sem.at[RECV[phase]]).wait)
 
     def finish_gram(side, phase):
-        wait_owned(recv_sem, phase + 1, gram_all.at[side])
+        wait_owned(phase + 1, gram_all.at[side])
         for c in range(chunks):
             gram_scr[c * rows : (c + 1) * rows, :] = gram_all[side, c]
         folded = gram_scr[...]
@@ -320,12 +322,10 @@
     start_gram(1, right_t)
     tiles_load.wait()
 
-    wait_all(recv_sem, 0, v_all)
+    wait_all(0, v_all)
     v_table[0 : devices * pad_tiles, :] = (
         v_all[...].reshape(devices * pad_tiles, LANES).astype(jnp.float32)
     )
-    dots = jnp.zeros((SUB, LANES), jnp.float32)
-    square = jnp.zeros((SUB, LANES), jnp.float32)
     for r in range(blocks):
         if r == blocks - 1:
             share_gram(0, 1)
@@ -336,7 +336,11 @@
                 col = col // own_tiles * pad_tiles + lax.rem(col, own_tiles)
             col = jnp.where(s < count_s[r], col, devices * pad_tiles)
             total = total + tiles[r, s].astype(jnp.float32) * v_table[pl.ds(col, 1), :]
-        p_col = jnp.broadcast_to(jnp.sum(total, axis=1, keepdims=True), (LANES, LANES))
+        p_scr[r] = total
+    dots = jnp.zeros((SUB, LANES), jnp.float32)
+    square = jnp.zeros((SUB, LANES), jnp.float32)
+    for r in range(blocks):
+        p_col = jnp.broadcast_to(jnp.sum(p_scr[r], axis=1, keepdims=True), (LANES, LANES))
         p_scr[r] = p_col
         dots = dots + fold(left[r * LANES : (r + 1) * LANES, :] * p_col)
         square = square + fold(p_col * p_col)
@@ -350,7 +354,7 @@
 
     def finish_dots(side, phase):
         gram = finish_gram(side, phase)
-        wait_all(recv_sem, 3 + side, dot_recv.at[side])
+        wait_all(3 + side, dot_recv.at[side])
         both = jnp.sum(dot_recv[side], axis=0)
         first, square = both[0:1, :], both[1:2, 0:1]
         lane = lax.broadcasted_iota(jnp.int32, (1, keep), 1)
@@ -360,15 +364,15 @@
         coef_row = to_row(coef)
         spread = jnp.sum(gram * coef, axis=0, keepdims=True)
         change = jnp.sum(coef_row * (spread - 2.0 * first), axis=1, keepdims=True)
-        return coef, coef_row, jnp.sqrt(square + change + 1e-06)
+        return coef, coef_row, square + change + 1e-06
 
     start_dots(
         0, jnp.sum(dots, axis=0, keepdims=True), jnp.sum(square, axis=0, keepdims=True)
     )
     send_gram(1, 6)
 
-    coef, coef_row, alpha = finish_dots(0, 1)
-    inverse = 1.0 / alpha
+    coef, coef_row, total = finish_dots(0, 1)
+    inverse, alpha = lax.rsqrt(total), jnp.sqrt(total)
 
     for r in range(blocks):
         fix = jnp.sum(left[r * LANES : (r + 1) * LANES, :] * coef_row, axis=1, keepdims=True)
@@ -406,7 +410,7 @@
     send_all(5, lambda other: part_send.at[other], part_recv)
     for r in range(blocks):
         out_ref[own_tiles + r : own_tiles + r + 1, :] = to_row(p_scr[r]) * left_scale
-    wait_all(recv_sem, 5, part_recv)
+    wait_all(5, part_recv)
     share_gram(1, 6)
     unit = jnp.exp2(part_recv[:, words:, :].astype(jnp.float32))
     word = part_recv[:, 0:words, :]
@@ -422,23 +426,25 @@
     dots = to_row(jnp.sum(total, axis=1, keepdims=True))
     square = jnp.sum(r_vec * r_vec, keepdims=True)
     start_dots(1, dots, jnp.broadcast_to(square, (1, LANES)))
-    coef, coef_row, beta_new = finish_dots(1, 6)
+    coef, coef_row, total = finish_dots(1, 6)
+    beta_new = jnp.sqrt(total)
     place = lax.broadcasted_iota(jnp.int32, (1, LANES), 1)
     out_ref[own_tiles + blocks : own_tiles + blocks + 1, :] = jnp.where(
         place == 0, alpha, beta_new
     )
-    inverse = right_scale / beta_new
+    inverse = right_scale * lax.rsqrt(total)
     for t in range(own_tiles):
         fix = jnp.sum(right_t[:, t * LANES : (t + 1) * LANES] * coef, axis=0, keepdims=True)
         out_ref[t : t + 1, :] = (r_vec[t : t + 1, :] - fix) * inverse
 
-    wait_all(send_sem, 0, v_all)
-    for phase, side in ((1, 0), (6, 1)):
-        wait_owned(send_sem, phase, gram_all.at[side])
-        pl.when(owner)(functools.partial(wait_all, send_sem, phase + 1, gram_recv.at[side]))
-    wait_all(send_sem, 3, dot_recv.at[0])
-    wait_all(send_sem, 4, dot_recv.at[1])
-    wait_all(send_sem, 5, part_recv)
+    each = v_send.shape[0] // 2 + 2 * dot_send.shape[1] + part_send.shape[1]
+    grams = 2 * rows
+    for mine, size in (
+        (owner, (devices - 1) * (each + grams) + (owners - 1) * grams),
+        (jnp.logical_not(owner), (devices - 1) * each + owners * grams),
+    ):
+        most = sent.at[pl.ds(0, size)]
+        pl.when(mine)(pltpu.make_async_copy(most, most, send_sem.at[0]).wait)
 
 
 def place_kernel(own_tiles, blocks, packed, out_left, out_right, out_coef):
@@ -465,6 +471,8 @@
     while (blocks * stride) % LANES:
         stride += 8
     entries = blocks * stride
+    sent_rows = (devices - 1) * (pad_tiles // 2 + 4 + part_rows // 2 + 1 + 2 * rows)
+    sent_rows += owners * 2 * rows
     f32, bf16, i32 = jnp.float32, jnp.bfloat16, jnp.int32
     vmem = pl.BlockSpec(memory_space=pltpu.VMEM)
     hbm = pl.BlockSpec(memory_space=pl.ANY)
@@ -510,9 +518,10 @@
             pltpu.VMEM((2, devices, 2, keep), f32),
             pltpu.VMEM((devices, part_rows // 2 + 1, LANES), i32),
             pltpu.VMEM((devices, part_rows // 2 + 1, LANES), i32),
+            pltpu.VMEM((sent_rows, LANES), f32),
             pltpu.SemaphoreType.DMA((9,)),
-            pltpu.SemaphoreType.DMA((8,)),
-            pltpu.SemaphoreType.DMA((8,)),
+            pltpu.SemaphoreType.DMA((1,)),
+            pltpu.SemaphoreType.DMA((5,)),
         ],
         compiler_params=pltpu.CompilerParams(
             collective_id=0, has_side_effects=True, vmem_limit_bytes=MAIN_VMEM - 512 * (-(-(own_tiles + blocks + 1) // SUB) * SUB)

time: 31.2 us -> 30.4 us (0.974)
  Pallas kernels: 29.7 us -> 28.9 us
    pallas_call x1, Pallas kernels: 29.1 us -> 28.3 us  [on_device(): pl.pallas_call(functools.partial(steps_kernel, blks, planes, own_tiles, m...]
where the time goes in v5:
time: 30.4 us; the launch traced here: 30.2 us
  Pallas kernels  28.9 us (95%)
  between operations  1.29 us (4%)
    pallas_call x1, Pallas kernels, on_device(): pl.pallas_call(functools.partial(steps_kernel, blks, planes, own_tiles, m...  28.3 us
    pallas_call x1, Pallas kernels, on_device(): pl.pallas_call(functools.partial(place_kernel, own_tiles, blocks), out_sh...  0.61 us

profile of v5, /device:TPU:0, one launch (start us, length us, event | category | flops | bytes accessed | tf_op | source)
XLA Modules:
  0.0 30.2 jit_solution(15601327987178004712)
XLA Ops:
  1.3 28.3 %shard_map.103.packed = f32[21,128]{1,0:T(8,128)S(1)} custom-call(f32[1]{0:T(128)S(6)} %copy.11.beta_hbm, s32[4]{0:T(128)} %count_hbm.1, s32[4,24]{1,0:T(4,128)} %cols_hbm.1, f32[4,128]{1,0:T(4,128)} %bitcast.3, f32[16,128]{1,0:T(8,128)} %bitcast.2, bf16[4,24,128,128]{3,2,1,0:T(8,128)(2,1)} %tiles_hbm.1, f32[512,128]{1,0:T(8,128)} %left_hbm.1, ...), custom_call_target="tpu_custom_call" | custom-call | tf_op jit(solution)/shard_map/pallas_call | solution.py:479
  29.6 0.6 %shard_map.104 = (f32[1,512]{1,0:T(1,128)}, f32[1,2048]{1,0:T(1,128)}, f32[2]{0:T(128)}) custom-call(f32[21,128]{1,0:T(8,128)S(1)} %shard_map.103.packed), custom_call_target="tpu_custom_call" | custom-call | tf_op jit(solution)/shard_map/pallas_call | solution.py:539

commit v6 on v5

--- a/solution.py
+++ b/solution.py
@@ -226,14 +226,15 @@
 
         if unrolled:
             near = flips(lax.rem(me_blk, owner_blks), owner_blks)
-            for k in reversed(range(owner_blks)):
-                for p in reversed(range(planes)):
-                    part = near[k] * planes + plane_of[p]
-                    place = (first_owner + near[k], plane_of[p])
-                    if k == first_owner and p == 0:
-                        pl.when(jnp.logical_not(owner))(functools.partial(send, part, place))
-                    else:
-                        send(part, place)
+            weight = lambda m: m[0] % 2 + m[1] // 2 + 0.3 * (m[1] % 2) + 0.6 * (m[0] // 2)
+            pairs = [(k, p) for k in range(owner_blks) for p in range(planes)]
+            for k, p in sorted(pairs, key=weight, reverse=True):
+                part = near[k] * planes + plane_of[p]
+                place = (first_owner + near[k], plane_of[p])
+                if k == first_owner and p == 0:
+                    pl.when(jnp.logical_not(owner))(functools.partial(send, part, place))
+                else:
+                    send(part, place)
             return
 
         def body(step, carry):
@@ -369,6 +370,7 @@
     start_dots(
         0, jnp.sum(dots, axis=0, keepdims=True), jnp.sum(square, axis=0, keepdims=True)
     )
+    pl.delay(1900)
     send_gram(1, 6)
 
     coef, coef_row, total = finish_dots(0, 1)

time: 30.4 us -> 30.3 us (level)
  no operation moved by 1% of the time
where the time goes in v6:
time: 30.3 us; the launch traced here: 30 us
  Pallas kernels  28.8 us (95%)
  between operations  1.29 us (4%)
    pallas_call x1, Pallas kernels, on_device(): pl.pallas_call(functools.partial(steps_kernel, blks, planes, own_tiles, m...  28.1 us
    pallas_call x1, Pallas kernels, on_device(): pl.pallas_call(functools.partial(place_kernel, own_tiles, blocks), out_sh...  0.61 us

profile of v6, /device:TPU:0, one launch (start us, length us, event | category | flops | bytes accessed | tf_op | source)
XLA Modules:
  0.0 30.0 jit_solution(13618434760144159632)
XLA Ops:
  1.3 28.1 %shard_map.103.packed = f32[21,128]{1,0:T(8,128)S(1)} custom-call(f32[1]{0:T(128)S(6)} %copy.11.beta_hbm, s32[4]{0:T(128)} %count_hbm.1, s32[4,24]{1,0:T(4,128)} %cols_hbm.1, f32[4,128]{1,0:T(4,128)} %bitcast.3, f32[16,128]{1,0:T(8,128)} %bitcast.2, bf16[4,24,128,128]{3,2,1,0:T(8,128)(2,1)} %tiles_hbm.1, f32[512,128]{1,0:T(8,128)} %left_hbm.1, ...), custom_call_target="tpu_custom_call" | custom-call | tf_op jit(solution)/shard_map/pallas_call | solution.py:481
  29.4 0.6 %shard_map.104 = (f32[1,512]{1,0:T(1,128)}, f32[1,2048]{1,0:T(1,128)}, f32[2]{0:T(128)}) custom-call(f32[21,128]{1,0:T(8,128)S(1)} %shard_map.103.packed), custom_call_target="tpu_custom_call" | custom-call | tf_op jit(solution)/shard_map/pallas_call | solution.py:541
